TPU v7x, 256 devices: a whole 4x4x8 slice. The times are simulated.
256 devices in a mesh: gx: 8 (over y, core), gy: 16 (over z, x_lo), gz: 2 (over x_hi).
Axes of the slice: x: 4 (x_hi: 2, x_lo: 2; x = x_hi * 2 + x_lo), y: 4, z: 8, core: 2. Of those that a mesh axis runs over, the one named last changes fastest.
Arguments:
- directions: float32 [8, 128, 256, 256], P(None, 'gx', 'gy', 'gz'), may hold values from -6 to 6
- state: float32 [128, 256, 256], P('gx', 'gy', 'gz'), may hold values from -2 to 2
- log_cond: float32 [128, 256, 256], P('gx', 'gy', 'gz'), may hold values from -1 to 1
- obs_mask: int32 [128, 256, 256], P('gx', 'gy', 'gz'), may hold values 0 or 1
Outputs:
- hessian_action: float32 [8, 128, 256, 256], P(None, 'gx', 'gy', 'gz')
- quotient: float32 [8], replicated
All inputs are finite; a program needn't handle non-finite values. No bound on the sum of `obs_mask` on one device may be relied on, other than what follows from the above.
Results may differ from a plain program's by a relative error of at most 0.00002.
Values sent between devices are 32-bit elements; how exact they have to be, the bound alone decides.
A program may use at most 128 MiB of HBM per device.

v0:
```python
import math
import jax
import jax.numpy as jnp
from jax import lax
from jax.sharding import Mesh
from jax.sharding import PartitionSpec as P

ITERS = 4
GX_GY_GZ = ("gx_0", "gx_1", "gy_0", "gy_1", "gz")
GX = ("gx_0", "gx_1")
GY = ("gy_0", "gy_1")
SHIFT = 0.3
BETA = 0.05
DATA_WEIGHT = 10.0


def with_halo(shard, sides, width):
    for axis, dim in sides:
        size, length = (lax.axis_size(axis), shard.shape[dim])
        up = [(i, (i + 1) % size) for i in range(size - 1)]
        down = [(j, i) for i, j in up]
        last = lax.slice_in_dim(shard, length - width, length, axis=dim)
        leading = lax.slice_in_dim(shard, 0, width, axis=dim)
        before = lax.ppermute(last, axis, up)
        after = lax.ppermute(leading, axis, down)
        shard = jnp.concatenate([before, shard, after], axis=dim)
    return shard


def over_axes(shard, axes):
    for axis in axes:
        shard = lax.psum(shard, axis)
    return shard


def chebyshev(count):
    return [
        1.0 / (1.125 + 0.825 * math.cos(math.pi * (2 * j + 1) / (2 * count))) for j in range(count)
    ]


def neighbours(padded):
    total = padded[..., 2:, 1:-1, 1:-1] + padded[..., :-2, 1:-1, 1:-1]
    total = total + padded[..., 1:-1, 2:, 1:-1] + padded[..., 1:-1, :-2, 1:-1]
    return total + padded[..., 1:-1, 1:-1, 2:] + padded[..., 1:-1, 1:-1, :-2]


def trim_rim(field, layers):
    return field[..., layers:-layers, layers:-layers, layers:-layers]


def trim_to(field, layers):
    if layers == 0:
        return field
    return trim_rim(field, layers)


def shards(directions, state, log_cond, obs_mask):
    cheb_w = chebyshev(ITERS)
    conduct = jnp.exp(log_cond)
    observed = obs_mask.astype(jnp.float32)
    outer = ITERS - 1
    stacked = jnp.concatenate([state[None], conduct[None], directions], axis=0)
    padded = with_halo(stacked, ((GX, 1), (GY, 2), ("gz", 3)), ITERS)
    state_wide = padded[0]
    conduct_wide = trim_rim(padded[1], 1)
    diagonal_wide = SHIFT + 6.0 * conduct_wide
    delta_wide = padded[2:]
    lap_wide = 6.0 * trim_rim(state_wide, 1) - neighbours(state_wide)
    source_wide = -conduct_wide * trim_rim(delta_wide, 1) * lap_wide
    tangent = cheb_w[0] * source_wide / diagonal_wide
    margin = outer
    for step in range(1, ITERS):
        margin = margin - 1
        cut = outer - margin
        inner = trim_rim(tangent, 1)
        cond_here = trim_to(conduct_wide, cut)
        diag_here = trim_to(diagonal_wide, cut)
        applied = diag_here * inner - cond_here * neighbours(tangent)
        tangent = inner + cheb_w[step] * (trim_to(source_wide, cut) - applied) / diag_here
    data_rhs = DATA_WEIGHT * observed * tangent
    rhs_wide = with_halo(data_rhs, ((GX, 1), (GY, 2), ("gz", 3)), outer)
    adjoint = cheb_w[0] * rhs_wide / diagonal_wide
    margin = outer
    for step in range(1, ITERS):
        flux = trim_to(conduct_wide, outer - margin) * adjoint
        margin = margin - 1
        cut = outer - margin
        inner = trim_rim(adjoint, 1)
        diag_here = trim_to(diagonal_wide, cut)
        applied = diag_here * inner - neighbours(flux)
        adjoint = inner + cheb_w[step] * (trim_to(rhs_wide, cut) - applied) / diag_here
    lap_state = trim_to(lap_wide, outer)
    delta_pad = trim_to(delta_wide, outer)
    hessian_action = -conduct * lap_state * adjoint + BETA * (
        6.0 * directions - neighbours(delta_pad)
    )
    cells = (
        directions.shape[1]
        * directions.shape[2]
        * directions.shape[3]
        * lax.axis_size(GX)
        * lax.axis_size(GY)
        * lax.axis_size("gz")
    )
    partial_sums = jnp.sum(directions * hessian_action, axis=(1, 2, 3))
    quotient = over_axes(partial_sums, GX_GY_GZ) / cells
    return (hessian_action, quotient)


def solution(mesh):
    torus = Mesh(
        mesh.devices.reshape(4, 2, 8, 2, mesh.shape["gz"]), ("gx_0", "gx_1", "gy_0", "gy_1", "gz")
    )
    placed = (P(None, GX, GY, "gz"), P(GX, GY, "gz"), P(GX, GY, "gz"), P(GX, GY, "gz"))
    return jax.shard_map(
        shards, mesh=torus, in_specs=placed, out_specs=(P(None, GX, GY, "gz"), P()), check_vma=False
    )
```

profile of v0, /device:TPU:6, one launch (start us, length us, event | category | flops | bytes accessed | tf_op | source)
XLA Modules:
  0.0 248.0 jit_solution(18383695558841984095)
XLA Ops:
  2.7 1.9 collective-permute-start
  4.6 1.3 collective-permute-start.1
  6.0 3.5 %collective-permute-done.1 = f32[10,4,16,128]{3,2,1,0:T(8,128)S(1)} collective-permute-done((f32[10,4,16,128]{3,2,1,0:T(8,128)S(1)}, f32[10,4,16,128]{3,2,1,0:T(8,128)S(1)}, u32[]{:S(2)}, u32[]{:S(2)}) %collective-permute-start.1) | collective-permute-done | bytes 327712 | tf_op jit(solution)/shard_map/ppermute | solution.py:25
  9.5 1.5 pad_maximum_fusion.24
  11.1 2.7 %collective-permute-start.3 = (f32[10,24,4,128]{3,1,2,0:T(8,128)S(1)}, f32[10,24,4,128]{3,1,2,0:T(8,128)S(1)}, u32[]{:S(2)}, u32[]{:S(2)}) collective-permute-start(f32[10,24,4,128]{3,1,2,0:T(8,128)S(1)} %copy.40), channel_id=1, source_target_pairs={{2,0},{4,2},{6,4},{8,6},{10,8},{12,10},{14,12},{16,14},{18,16},{20... | collective-permute-start | bytes 1474568 | tf_op jit(solution)/shard_map/ppermute | solution.py:25
  13.9 4.0 %collective-permute-start.2 = (f32[10,24,4,128]{3,1,2,0:T(8,128)S(1)}, f32[10,24,4,128]{3,1,2,0:T(8,128)S(1)}, u32[]{:S(2)}, u32[]{:S(2)}) collective-permute-start(f32[10,24,4,128]{3,1,2,0:T(8,128)S(1)} %copy.39), channel_id=1, source_target_pairs={{0,2},{2,4},{4,6},{6,8},{8,10},{10,12},{12,14},{14,16},{16,18},{18... | collective-permute-start | bytes 1474568 | tf_op jit(solution)/shard_map/ppermute | solution.py:24
  17.9 5.8 %collective-permute-done.3 = f32[10,24,4,128]{3,1,2,0:T(8,128)S(1)} collective-permute-done((f32[10,24,4,128]{3,1,2,0:T(8,128)S(1)}, f32[10,24,4,128]{3,1,2,0:T(8,128)S(1)}, u32[]{:S(2)}, u32[]{:S(2)}) %collective-permute-start.3) | collective-permute-done | bytes 491552 | tf_op jit(solution)/shard_map/ppermute | solution.py:25
  23.9 14.6 %collective-permute-done.2 = f32[10,24,4,128]{3,1,2,0:T(8,128)S(1)} collective-permute-done((f32[10,24,4,128]{3,1,2,0:T(8,128)S(1)}, f32[10,24,4,128]{3,1,2,0:T(8,128)S(1)}, u32[]{:S(2)}, u32[]{:S(2)}) %collective-permute-start.2) | collective-permute-done | bytes 491552 | tf_op jit(solution)/shard_map/ppermute | solution.py:24
  39.9 2.6 %fusion.63 = (f32[10,24,24,4]{3,2,1,0:T(8,128)}, f32[10,24,24,4]{3,2,1,0:T(8,128)S(1)}) fusion(f32[10,24,24,128]{3,2,1,0:T(8,128)S(1)} %pad_maximum_fusion.2), kind=kLoop, calls=%fused_computation.145 | loop fusion | bytes 368640 | tf_op jit(solution)/shard_map/slice | solution.py:23
  42.5 3.7 %copy.44 = f32[10,24,24,4]{2,1,3,0:T(8,128)} copy(f32[10,24,24,4]{3,2,1,0:T(8,128)} %get-tuple-element.17) | data formatting | bytes 184320 | tf_op jit(solution)/shard_map/slice | solution.py:23
  46.2 2.5 %copy.43 = f32[10,24,24,4]{2,1,3,0:T(8,128)} copy(f32[10,24,24,4]{3,2,1,0:T(8,128)S(1)} %get-tuple-element.18) | data formatting | bytes 184320 | tf_op jit(solution)/shard_map/slice | solution.py:22
  49.9 7.9 %collective-permute-start.5 = (f32[10,24,24,4]{2,1,3,0:T(8,128)}, f32[10,24,24,4]{2,1,3,0:T(8,128)}, u32[]{:S(2)}, u32[]{:S(2)}) collective-permute-start(f32[10,24,24,4]{2,1,3,0:T(8,128)} %copy.44), channel_id=1, source_target_pairs={{1,0},{3,2},{5,4},{7,6},{9,8},{11,10},{13,12},{15,14},{17,16},{19,... | collective-permute-start | bytes 276488 | tf_op jit(solution)/shard_map/ppermute | solution.py:25
  57.9 1.6 convert_multiply_fusion
  59.4 8.2 %collective-permute-done.5 = f32[10,24,24,4]{2,1,3,0:T(8,128)} collective-permute-done((f32[10,24,24,4]{2,1,3,0:T(8,128)}, f32[10,24,24,4]{2,1,3,0:T(8,128)}, u32[]{:S(2)}, u32[]{:S(2)}) %collective-permute-start.5) | collective-permute-done | bytes 92192 | tf_op jit(solution)/shard_map/ppermute | solution.py:25
  67.6 2.5 %copy.46 = f32[10,24,24,4]{3,2,1,0:T(8,128)S(1)} copy(f32[10,24,24,4]{2,1,3,0:T(8,128)} %collective-permute-done.5) | data formatting | bytes 184320 | tf_op jit(solution)/shard_map/ppermute | solution.py:25
  70.1 3.9 %copy.45 = f32[10,24,24,4]{3,2,1,0:T(8,128)} copy(f32[10,24,24,4]{2,1,3,0:T(8,128)} %collective-permute-done.4) | data formatting | bytes 184320 | tf_op jit(solution)/shard_map/ppermute | solution.py:24
  74.0 8.5 %pad_maximum_fusion = f32[10,24,24,136]{3,2,1,0:T(8,128)S(1)} fusion(f32[10,24,24,4]{3,2,1,0:T(8,128)S(1)} %copy.46, f32[10,24,4,128]{3,2,1,0:T(4,128)S(1)} %copy.42, f32[10,4,16,128]{3,2,1,0:T(8,128)} %copy-done.12, f32[8,16,16,128]{3,2,1,0:T(8,128)} %param.4, f32[1,16,16,128]{3,2,1,0:T(8,128)} %copy-done.14, f32[1,16,16,128]{3,2,1,0:T(8,128)} %bitcast.9, ...), kind=kLoop, calls=%fused_computation | loop fusion | flops 6266880 | bytes 6266880 | tf_op jit(solution)/shard_map/concatenate | solution.py:26
  83.1 1.8 fusion.66
  85.5 1.4 multiply_divide_fusion.1
  87.0 7.5 %fusion.11 = f32[8,20,20,132]{3,2,1,0:T(8,128)S(1)} fusion(f32[8,22,22,134]{3,2,1,0:T(8,128)S(1)} %get-tuple-element.13, f32[8,22,22,134]{3,2,1,0:T(8,128)S(1)} %get-tuple-element.14, f32[20,20,132]{2,1,0:T(8,128)S(1)} %slice.379, f32[20,20,132]{2,1,0:T(8,128)S(1)} %slice.378), kind=kLoop, calls=%fused_computation.26 | loop fusion | flops 5068800 | bytes 15628800 | tf_op jit(solution)/shard_map/add | solution.py:80
  94.5 7.3 %fusion.22 = f32[8,18,18,130]{3,2,1,0:T(8,128)S(1)} fusion(f32[8,20,20,132]{3,2,1,0:T(8,128)S(1)} %fusion.11, f32[8,22,22,134]{3,2,1,0:T(8,128)S(1)} %get-tuple-element.14, f32[18,18,130]{2,1,0:T(8,128)S(1)} %slice.389, f32[18,18,130]{2,1,0:T(8,128)S(1)} %slice.388), kind=kLoop, calls=%fused_computation.47 | loop fusion | flops 4043520 | bytes 12467520 | tf_op jit(solution)/shard_map/add | solution.py:80
  101.9 2.9 %fusion.57 = f32[8,16,16,128]{3,2,1,0:T(8,128)} fusion(f32[8,18,18,130]{3,2,1,0:T(8,128)S(1)} %fusion.22, f32[8,22,22,134]{3,2,1,0:T(8,128)S(1)} %get-tuple-element.14, f32[16,16,128]{2,1,0:T(8,128)S(1)} %slice.399, f32[16,16,128]{2,1,0:T(8,128)S(1)} %slice.398, f32[16,16,128]{2,1,0:T(8,128)S(1)} %copy-done.33), kind=kLoop, calls=%fused_computation.118 | loop fusion | flops 3407872 | bytes 9830400 | tf_op jit(solution)/shard_map/mul | solution.py:81
  105.9 1.3 collective-permute-start.6
  107.2 1.3 collective-permute-start.7
  108.6 7.4 %collective-permute-done.7 = f32[8,3,16,128]{3,2,1,0:T(8,128)S(1)} collective-permute-done((f32[8,3,16,128]{3,2,1,0:T(8,128)S(1)}, f32[8,3,16,128]{3,2,1,0:T(8,128)S(1)}, u32[]{:S(2)}, u32[]{:S(2)}) %collective-permute-start.7) | collective-permute-done | bytes 196640 | tf_op jit(solution)/shard_map/ppermute | solution.py:25
  115.9 1.4 pad_maximum_fusion.27
  117.4 1.9 collective-permute-start.9
  119.4 4.8 %collective-permute-start.8 = (f32[8,22,3,128]{3,0,2,1:T(8,128)S(1)}, f32[8,22,3,128]{3,0,2,1:T(8,128)S(1)}, u32[]{:S(2)}, u32[]{:S(2)}) collective-permute-start(f32[8,22,3,128]{3,0,2,1:T(8,128)S(1)} %copy.47), channel_id=1, source_target_pairs={{0,2},{2,4},{4,6},{6,8},{8,10},{10,12},{12,14},{14,16},{16,18},{18... | collective-permute-start | bytes 811016 | tf_op jit(solution)/shard_map/ppermute | solution.py:24
  124.2 2.5 %collective-permute-done.9 = f32[8,22,3,128]{3,0,2,1:T(8,128)S(1)} collective-permute-done((f32[8,22,3,128]{3,0,2,1:T(8,128)S(1)}, f32[8,22,3,128]{3,0,2,1:T(8,128)S(1)}, u32[]{:S(2)}, u32[]{:S(2)}) %collective-permute-start.9) | collective-permute-done | bytes 270368 | tf_op jit(solution)/shard_map/ppermute | solution.py:25
  126.9 8.2 %collective-permute-done.8 = f32[8,22,3,128]{3,0,2,1:T(8,128)S(1)} collective-permute-done((f32[8,22,3,128]{3,0,2,1:T(8,128)S(1)}, f32[8,22,3,128]{3,0,2,1:T(8,128)S(1)}, u32[]{:S(2)}, u32[]{:S(2)}) %collective-permute-start.8) | collective-permute-done | bytes 270368 | tf_op jit(solution)/shard_map/ppermute | solution.py:24
  136.3 2.0 fusion.64
  138.3 1.8 copy.51
  140.2 2.8 %copy.52 = f32[8,22,22,3]{2,0,3,1:T(8,128)S(1)} copy(f32[8,22,22,3]{3,2,1,0:T(8,128)} %get-tuple-element.20) | data formatting | bytes 92928 | tf_op jit(solution)/shard_map/slice | solution.py:23
  143.0 5.9 %collective-permute-start.11 = (f32[8,22,22,3]{2,0,3,1:T(8,128)S(1)}, f32[8,22,22,3]{2,0,3,1:T(8,128)S(1)}, u32[]{:S(2)}, u32[]{:S(2)}) collective-permute-start(f32[8,22,22,3]{2,0,3,1:T(8,128)S(1)} %copy.52), channel_id=1, source_target_pairs={{1,0},{3,2},{5,4},{7,6},{9,8},{11,10},{13,12},{15,14},{17,16},{19,... | collective-permute-start | bytes 139400 | tf_op jit(solution)/shard_map/ppermute | solution.py:25
  148.9 1.3 collective-permute-start.10
  150.2 1.8 slice_multiply_fusion.2
  152.0 8.8 %collective-permute-done.10 = f32[8,22,22,3]{2,0,3,1:T(8,128)S(1)} collective-permute-done((f32[8,22,22,3]{2,0,3,1:T(8,128)}, f32[8,22,22,3]{2,0,3,1:T(8,128)S(1)}, u32[]{:S(2)}, u32[]{:S(2)}) %collective-permute-start.10) | collective-permute-done | bytes 46496 | tf_op jit(solution)/shard_map/ppermute | solution.py:24
  160.8 2.5 %copy.53 = f32[8,22,22,3]{3,2,1,0:T(8,128)} copy(f32[8,22,22,3]{2,0,3,1:T(8,128)S(1)} %collective-permute-done.10) | data formatting | bytes 92928 | tf_op jit(solution)/shard_map/ppermute | solution.py:24
  163.2 2.5 %copy.54 = f32[8,22,22,3]{3,2,1,0:T(8,128)} copy(f32[8,22,22,3]{2,0,3,1:T(8,128)S(1)} %collective-permute-done.11) | data formatting | bytes 92928 | tf_op jit(solution)/shard_map/ppermute | solution.py:25
  165.8 8.1 %broadcast_multiply_fusion = (f32[8,22,22,134]{3,2,1,0:T(8,128)S(1)}, f32[8,22,22,134]{3,2,1,0:T(8,128)}, f32[8,22,22,134]{3,2,1,0:T(8,128)S(1)}) fusion(f32[22,22,134]{2,1,0:T(8,128)} %get-tuple-element.29, f32[22,22,134]{2,1,0:T(8,128)S(1)} %copy-done.5, f32[8,22,22,3]{3,2,1,0:T(8,128)} %copy.54, f32[8,22,3,128]{3,2,1,0:T(4,128)S(1)} %copy-done.25, ...), kind=kLoop, calls=%fused_computation.54 | loop fusion | flops 4669632 | bytes 8820416 | tf_op jit(solution)/shard_map/mul | solution.py:86
  173.8 10.6 %broadcast_multiply_fusion.1 = (f32[8,20,20,132]{3,2,1,0:T(8,128)S(1)}, f32[8,20,20,132]{3,2,1,0:T(8,128)}) fusion(f32[20,20,132]{2,1,0:T(8,128)S(1)} %copy-done.17, f32[8,22,22,134]{3,2,1,0:T(8,128)S(1)} %get-tuple-element.10, f32[20,20,132]{2,1,0:T(8,128)S(1)} %copy-done.19, f32[8,22,22,134]{3,2,1,0:T(8,128)S(1)} %get-tuple-element.12, ...), kind=kLoop, calls=%fused_computation.55 | loop fusion | flops 5068800 | bytes 17318400 | tf_op jit(solution)/shard_map/mul | solution.py:86
  184.5 10.3 %broadcast_multiply_fusion.2 = (f32[8,18,18,130]{3,2,1,0:T(8,128)S(1)}, f32[8,18,18,130]{3,2,1,0:T(8,128)}) fusion(f32[18,18,130]{2,1,0:T(8,128)} %copy-done.20, f32[8,20,20,132]{3,2,1,0:T(8,128)S(1)} %get-tuple-element.8, f32[18,18,130]{2,1,0:T(8,128)} %copy-done.21, f32[8,22,22,134]{3,2,1,0:T(8,128)S(1)} %get-tuple-element.12, ...), kind=kLoop, calls=%fused_computation.56 | loop fusion | flops 4043520 | bytes 13815360 | tf_op jit(solution)/shard_map/mul | solution.py:86
  194.9 7.7 %multiply_reduce_fusion = (f32[8]{0:T(128)S(1)}, f32[8,16,16,128]{3,2,1,0:T(8,128)}) fusion(f32[8,16,16,128]{3,2,1,0:T(8,128)S(1)} %copy-done.3, f32[10,24,4,128]{3,2,1,0:T(4,128)S(1)} %copy-done.7, f32[10,4,16,128]{3,2,1,0:T(8,128)S(1)} %copy-done.13, f32[1,16,16,128]{3,2,1,0:T(8,128)S(1)} %copy-done.15, f32[1,16,16,128]{3,2,1,0:T(8,128)S(1)} %bitcast.11, ...), kind=kLoop, calls=%fused_computation.117 | loop fusion | flops 13893624 | bytes 12832800 | tf_op jit(solution)/shard_map/reduce_sum | solution.py:106
  202.6 11.8 %psum.35 = f32[8]{0:T(128)S(1)} all-reduce(f32[8]{0:T(128)S(1)} %get-tuple-element.4), channel_id=1, replica_groups=mesh['gx_0'=4,'gx_1'=2,'gy_0'=8,'gy_1'=2,'gz'=2] {'gx_0'}, use_global_device_ids=true, to_apply=%region_1.0 | all-reduce | flops 8 | bytes 64 | tf_op jit(solution)/shard_map/psum | solution.py:32
  214.4 2.5 psum.36
  216.8 19.1 %psum.37 = f32[8]{0:T(128)S(1)} all-reduce(f32[8]{0:T(128)S(1)} %psum.36), channel_id=1, replica_groups=mesh['gx_0'=4,'gx_1'=2,'gy_0'=8,'gy_1'=2,'gz'=2] {'gy_0'}, use_global_device_ids=true, to_apply=%region_3.0 | all-reduce | flops 8 | bytes 64 | tf_op jit(solution)/shard_map/psum | solution.py:32
  235.9 4.9 %psum.38 = f32[8]{0:T(128)S(1)} all-reduce(f32[8]{0:T(128)S(1)} %psum.37), channel_id=1, replica_groups=mesh['gx_0'=4,'gx_1'=2,'gy_0'=8,'gy_1'=2,'gz'=2] {'gy_1'}, use_global_device_ids=true, to_apply=%region_4.0 | all-reduce | flops 8 | bytes 64 | tf_op jit(solution)/shard_map/psum | solution.py:32
  240.8 6.4 %psum.39 = f32[8]{0:T(128)S(1)} all-reduce(f32[8]{0:T(128)S(1)} %psum.38), channel_id=1, replica_groups=mesh['gx_0'=4,'gx_1'=2,'gy_0'=8,'gy_1'=2,'gz'=2] {'gz'}, use_global_device_ids=true, to_apply=%region_5.0 | all-reduce | flops 8 | bytes 64 | tf_op jit(solution)/shard_map/psum | solution.py:32
  (94 shorter events, 9.2 us)
Async XLA Ops:
  1.6 37.0 %copy-start.14 = (f32[1,16,16,128]{3,2,1,0:T(8,128)}, f32[1,16,16,128]{3,2,1,0:T(8,128)S(1)}, u32[]{:S(2)}) copy-start(f32[1,16,16,128]{3,2,1,0:T(8,128)S(1)} %exponential_bitcast_fusion) | copy-start | bytes 393220
  2.7 36.7 %copy-start.2 = (f32[8,16,16,128]{3,2,1,0:T(8,128)S(1)}, f32[8,16,16,128]{3,2,1,0:T(8,128)}, u32[]{:S(2)}) copy-start(f32[8,16,16,128]{3,2,1,0:T(8,128)} %param.4) | copy-start | bytes 3145732
  2.7 36.6 %copy-start.22 = (f32[16,16,128]{2,1,0:T(8,128)S(1)}, f32[16,16,128]{2,1,0:T(8,128)}, u32[]{:S(2)}) copy-start(f32[16,16,128]{2,1,0:T(8,128)} %param.5) | copy-start | bytes 393220
  2.7 3.2 %collective-permute-start = (f32[10,4,16,128]{3,2,1,0:T(8,128)S(1)}, f32[10,4,16,128]{3,2,1,0:T(8,128)S(1)}, u32[]{:S(2)}, u32[]{:S(2)}) collective-permute-start(f32[10,4,16,128]{3,2,1,0:T(8,128)S(1)} %get-tuple-element.25), channel_id=1, source_target_pairs={{0,32},{32,64},{64,96},{96,128},{128,160},{160,192},{192,224},{1,3... | collective-permute-start | bytes 983048 | tf_op jit(solution)/shard_map/ppermute | solution.py:24
  4.6 4.9 %collective-permute-start.1 = (f32[10,4,16,128]{3,2,1,0:T(8,128)S(1)}, f32[10,4,16,128]{3,2,1,0:T(8,128)S(1)}, u32[]{:S(2)}, u32[]{:S(2)}) collective-permute-start(f32[10,4,16,128]{3,2,1,0:T(8,128)S(1)} %get-tuple-element.26), channel_id=1, source_target_pairs={{32,0},{64,32},{96,64},{128,96},{160,128},{192,160},{224,192},{33,... | collective-permute-start | bytes 983048 | tf_op jit(solution)/shard_map/ppermute | solution.py:25
  5.9 33.9 %copy-start.10 = (f32[10,4,16,128]{3,2,1,0:T(8,128)}, f32[10,4,16,128]{3,2,1,0:T(8,128)S(1)}, u32[]{:S(2)}) copy-start(f32[10,4,16,128]{3,2,1,0:T(8,128)S(1)} %collective-permute-done) | copy-start | bytes 983044
  9.5 30.4 %copy-start.12 = (f32[10,4,16,128]{3,2,1,0:T(8,128)}, f32[10,4,16,128]{3,2,1,0:T(8,128)S(1)}, u32[]{:S(2)}) copy-start(f32[10,4,16,128]{3,2,1,0:T(8,128)S(1)} %collective-permute-done.1) | copy-start | bytes 983044
  11.1 12.6 %collective-permute-start.3 = (f32[10,24,4,128]{3,1,2,0:T(8,128)S(1)}, f32[10,24,4,128]{3,1,2,0:T(8,128)S(1)}, u32[]{:S(2)}, u32[]{:S(2)}) collective-permute-start(f32[10,24,4,128]{3,1,2,0:T(8,128)S(1)} %copy.40), channel_id=1, source_target_pairs={{2,0},{4,2},{6,4},{8,6},{10,8},{12,10},{14,12},{16,14},{18,16},{20... | collective-permute-start | bytes 1474568 | tf_op jit(solution)/shard_map/ppermute | solution.py:25
  13.9 24.5 %collective-permute-start.2 = (f32[10,24,4,128]{3,1,2,0:T(8,128)S(1)}, f32[10,24,4,128]{3,1,2,0:T(8,128)S(1)}, u32[]{:S(2)}, u32[]{:S(2)}) collective-permute-start(f32[10,24,4,128]{3,1,2,0:T(8,128)S(1)} %copy.39), channel_id=1, source_target_pairs={{0,2},{2,4},{4,6},{6,8},{8,10},{10,12},{12,14},{14,16},{16,18},{18... | collective-permute-start | bytes 1474568 | tf_op jit(solution)/shard_map/ppermute | solution.py:24
  23.9 50.2 %copy-start.6 = (f32[10,24,4,128]{3,2,1,0:T(4,128)}, f32[10,24,4,128]{3,2,1,0:T(4,128)S(1)}, u32[]{:S(2)}) copy-start(f32[10,24,4,128]{3,2,1,0:T(4,128)S(1)} %copy.42) | copy-start | bytes 1474564
  38.6 0.8 copy-start.8
  48.7 21.5 %collective-permute-start.4 = (f32[10,24,24,4]{2,1,3,0:T(8,128)}, f32[10,24,24,4]{2,1,3,0:T(8,128)}, u32[]{:S(2)}, u32[]{:S(2)}) collective-permute-start(f32[10,24,24,4]{2,1,3,0:T(8,128)} %copy.43), channel_id=1, source_target_pairs={{0,1},{2,3},{4,5},{6,7},{8,9},{10,11},{12,13},{14,15},{16,17},{18,... | collective-permute-start | bytes 276488 | tf_op jit(solution)/shard_map/ppermute | solution.py:24
  49.9 17.7 %collective-permute-start.5 = (f32[10,24,24,4]{2,1,3,0:T(8,128)}, f32[10,24,24,4]{2,1,3,0:T(8,128)}, u32[]{:S(2)}, u32[]{:S(2)}) collective-permute-start(f32[10,24,24,4]{2,1,3,0:T(8,128)} %copy.44), channel_id=1, source_target_pairs={{1,0},{3,2},{5,4},{7,6},{9,8},{11,10},{13,12},{15,14},{17,16},{19,... | collective-permute-start | bytes 276488 | tf_op jit(solution)/shard_map/ppermute | solution.py:25
  70.1 12.4 %copy-start.1 = (f32[10,24,24,4]{3,2,1,0:T(8,128)}, f32[10,24,24,4]{3,2,1,0:T(8,128)S(1)}, u32[]{:S(2)}) copy-start(f32[10,24,24,4]{3,2,1,0:T(8,128)S(1)} %copy.46) | copy-start | bytes 276484
  82.9 11.6 %copy-start.20 = (f32[18,18,130]{2,1,0:T(8,128)}, f32[18,18,130]{2,1,0:T(8,128)S(1)}, u32[]{:S(2)}) copy-start(f32[18,18,130]{2,1,0:T(8,128)S(1)} %slice.389) | copy-start | bytes 505444
  83.1 3.9 %copy-start.16 = (f32[20,20,132]{2,1,0:T(8,128)}, f32[20,20,132]{2,1,0:T(8,128)S(1)}, u32[]{:S(2)}) copy-start(f32[20,20,132]{2,1,0:T(8,128)S(1)} %slice.379) | copy-start | bytes 633604
  85.0 2.0 copy-start.4
  85.0 2.0 copy-start.28
  85.1 16.8 %copy-start.30 = (f32[16,16,128]{2,1,0:T(8,128)}, f32[16,16,128]{2,1,0:T(8,128)S(1)}, u32[]{:S(2)}) copy-start(f32[16,16,128]{2,1,0:T(8,128)S(1)} %slice.398) | copy-start | bytes 393220
  85.3 9.2 %copy-start.21 = (f32[18,18,130]{2,1,0:T(8,128)}, f32[18,18,130]{2,1,0:T(8,128)S(1)}, u32[]{:S(2)}) copy-start(f32[18,18,130]{2,1,0:T(8,128)S(1)} %slice.388) | copy-start | bytes 505444
  85.5 1.5 copy-start.18
  94.5 7.3 %copy-start.33 = (f32[16,16,128]{2,1,0:T(8,128)S(1)}, f32[16,16,128]{2,1,0:T(8,128)}, u32[]{:S(2)}) copy-start(f32[16,16,128]{2,1,0:T(8,128)} %convert_multiply_fusion) | copy-start | bytes 393220
  104.8 31.1 %copy-start = (f32[8,16,16,128]{3,2,1,0:T(8,128)S(1)}, f32[8,16,16,128]{3,2,1,0:T(8,128)}, u32[]{:S(2)}) copy-start(f32[8,16,16,128]{3,2,1,0:T(8,128)} %fusion.57) | copy-start | bytes 3145732
  105.9 2.6 %collective-permute-start.6 = (f32[8,3,16,128]{3,2,1,0:T(8,128)S(1)}, f32[8,3,16,128]{3,2,1,0:T(8,128)S(1)}, u32[]{:S(2)}, u32[]{:S(2)}) collective-permute-start(f32[8,3,16,128]{3,2,1,0:T(8,128)S(1)} %get-tuple-element.27), channel_id=1, source_target_pairs={{0,32},{32,64},{64,96},{96,128},{128,160},{160,192},{192,224},{1,3... | collective-permute-start | bytes 589832 | tf_op jit(solution)/shard_map/ppermute | solution.py:24
  107.2 8.7 %collective-permute-start.7 = (f32[8,3,16,128]{3,2,1,0:T(8,128)S(1)}, f32[8,3,16,128]{3,2,1,0:T(8,128)S(1)}, u32[]{:S(2)}, u32[]{:S(2)}) collective-permute-start(f32[8,3,16,128]{3,2,1,0:T(8,128)S(1)} %get-tuple-element.28), channel_id=1, source_target_pairs={{32,0},{64,32},{96,64},{128,96},{160,128},{192,160},{224,192},{33,... | collective-permute-start | bytes 589832 | tf_op jit(solution)/shard_map/ppermute | solution.py:25
  115.9 19.2 %copy-start.29 = (f32[8,3,16,128]{3,2,1,0:T(8,128)}, f32[8,3,16,128]{3,2,1,0:T(8,128)S(1)}, u32[]{:S(2)}) copy-start(f32[8,3,16,128]{3,2,1,0:T(8,128)S(1)} %collective-permute-done.7) | copy-start | bytes 589828
  117.4 9.4 %collective-permute-start.9 = (f32[8,22,3,128]{3,0,2,1:T(8,128)S(1)}, f32[8,22,3,128]{3,0,2,1:T(8,128)S(1)}, u32[]{:S(2)}, u32[]{:S(2)}) collective-permute-start(f32[8,22,3,128]{3,0,2,1:T(8,128)S(1)} %copy.48), channel_id=1, source_target_pairs={{2,0},{4,2},{6,4},{8,6},{10,8},{12,10},{14,12},{16,14},{18,16},{20... | collective-permute-start | bytes 811016 | tf_op jit(solution)/shard_map/ppermute | solution.py:25
  119.4 15.7 %collective-permute-start.8 = (f32[8,22,3,128]{3,0,2,1:T(8,128)S(1)}, f32[8,22,3,128]{3,0,2,1:T(8,128)S(1)}, u32[]{:S(2)}, u32[]{:S(2)}) collective-permute-start(f32[8,22,3,128]{3,0,2,1:T(8,128)S(1)} %copy.47), channel_id=1, source_target_pairs={{0,2},{2,4},{4,6},{6,8},{8,10},{10,12},{12,14},{14,16},{16,18},{18... | collective-permute-start | bytes 811016 | tf_op jit(solution)/shard_map/ppermute | solution.py:24
  126.9 8.3 %copy-start.24 = (f32[8,22,3,128]{3,2,1,0:T(4,128)}, f32[8,22,3,128]{3,2,1,0:T(4,128)S(1)}, u32[]{:S(2)}) copy-start(f32[8,22,3,128]{3,2,1,0:T(4,128)S(1)} %copy.50) | copy-start | bytes 811012
  135.2 0.7 copy-start.26
  140.2 25.6 %copy-start.5 = (f32[22,22,134]{2,1,0:T(8,128)S(1)}, f32[22,22,134]{2,1,0:T(8,128)}, u32[]{:S(2)}) copy-start(f32[22,22,134]{2,1,0:T(8,128)} %copy-done.4) | copy-start | bytes 778276
  140.2 25.6 %copy-start.25 = (f32[8,22,3,128]{3,2,1,0:T(4,128)S(1)}, f32[8,22,3,128]{3,2,1,0:T(4,128)}, u32[]{:S(2)}) copy-start(f32[8,22,3,128]{3,2,1,0:T(4,128)} %copy-done.24) | copy-start | bytes 811012
  140.2 25.6 %copy-start.27 = (f32[8,22,3,128]{3,2,1,0:T(4,128)S(1)}, f32[8,22,3,128]{3,2,1,0:T(4,128)}, u32[]{:S(2)}) copy-start(f32[8,22,3,128]{3,2,1,0:T(4,128)} %copy-done.26) | copy-start | bytes 811012
  143.0 20.2 %collective-permute-start.11 = (f32[8,22,22,3]{2,0,3,1:T(8,128)S(1)}, f32[8,22,22,3]{2,0,3,1:T(8,128)S(1)}, u32[]{:S(2)}, u32[]{:S(2)}) collective-permute-start(f32[8,22,22,3]{2,0,3,1:T(8,128)S(1)} %copy.52), channel_id=1, source_target_pairs={{1,0},{3,2},{5,4},{7,6},{9,8},{11,10},{13,12},{15,14},{17,16},{19,... | collective-permute-start | bytes 139400 | tf_op jit(solution)/shard_map/ppermute | solution.py:25
  148.9 11.8 %collective-permute-start.10 = (f32[8,22,22,3]{2,0,3,1:T(8,128)}, f32[8,22,22,3]{2,0,3,1:T(8,128)S(1)}, u32[]{:S(2)}, u32[]{:S(2)}) collective-permute-start(f32[8,22,22,3]{2,0,3,1:T(8,128)} %copy.51), channel_id=1, source_target_pairs={{0,1},{2,3},{4,5},{6,7},{8,9},{10,11},{12,13},{14,15},{16,17},{18,... | collective-permute-start | bytes 139400 | tf_op jit(solution)/shard_map/ppermute | solution.py:24
  165.8 8.1 %copy-start.17 = (f32[20,20,132]{2,1,0:T(8,128)S(1)}, f32[20,20,132]{2,1,0:T(8,128)}, u32[]{:S(2)}) copy-start(f32[20,20,132]{2,1,0:T(8,128)} %copy-done.16) | copy-start | bytes 633604
  165.8 8.1 %copy-start.19 = (f32[20,20,132]{2,1,0:T(8,128)S(1)}, f32[20,20,132]{2,1,0:T(8,128)}, u32[]{:S(2)}) copy-start(f32[20,20,132]{2,1,0:T(8,128)} %copy-done.18) | copy-start | bytes 633604
  184.5 10.4 %copy-start.3 = (f32[8,16,16,128]{3,2,1,0:T(8,128)S(1)}, f32[8,16,16,128]{3,2,1,0:T(8,128)}, u32[]{:S(2)}) copy-start(f32[8,16,16,128]{3,2,1,0:T(8,128)} %param.4) | copy-start | bytes 3145732
  184.5 10.4 %copy-start.7 = (f32[10,24,4,128]{3,2,1,0:T(4,128)S(1)}, f32[10,24,4,128]{3,2,1,0:T(4,128)}, u32[]{:S(2)}) copy-start(f32[10,24,4,128]{3,2,1,0:T(4,128)} %copy-done.6) | copy-start | bytes 1474564
  184.5 10.4 %copy-start.9 = (f32[10,24,4,128]{3,2,1,0:T(4,128)S(1)}, f32[10,24,4,128]{3,2,1,0:T(4,128)}, u32[]{:S(2)}) copy-start(f32[10,24,4,128]{3,2,1,0:T(4,128)} %copy-done.8) | copy-start | bytes 1474564
  184.5 10.4 %copy-start.11 = (f32[10,4,16,128]{3,2,1,0:T(8,128)S(1)}, f32[10,4,16,128]{3,2,1,0:T(8,128)}, u32[]{:S(2)}) copy-start(f32[10,4,16,128]{3,2,1,0:T(8,128)} %copy-done.10) | copy-start | bytes 983044
  184.5 10.4 %copy-start.13 = (f32[10,4,16,128]{3,2,1,0:T(8,128)S(1)}, f32[10,4,16,128]{3,2,1,0:T(8,128)}, u32[]{:S(2)}) copy-start(f32[10,4,16,128]{3,2,1,0:T(8,128)} %copy-done.12) | copy-start | bytes 983044
  184.5 10.4 %copy-start.15 = (f32[1,16,16,128]{3,2,1,0:T(8,128)S(1)}, f32[1,16,16,128]{3,2,1,0:T(8,128)}, u32[]{:S(2)}) copy-start(f32[1,16,16,128]{3,2,1,0:T(8,128)} %copy-done.14) | copy-start | bytes 393220
  184.5 10.4 %copy-start.23 = (f32[16,16,128]{2,1,0:T(8,128)S(1)}, f32[16,16,128]{2,1,0:T(8,128)}, u32[]{:S(2)}) copy-start(f32[16,16,128]{2,1,0:T(8,128)} %param.5) | copy-start | bytes 393220
  184.5 10.4 %copy-start.31 = (f32[16,16,128]{2,1,0:T(8,128)S(1)}, f32[16,16,128]{2,1,0:T(8,128)}, u32[]{:S(2)}) copy-start(f32[16,16,128]{2,1,0:T(8,128)} %copy-done.30) | copy-start | bytes 393220
  184.5 10.4 %copy-start.32 = (f32[16,16,128]{2,1,0:T(8,128)S(1)}, f32[16,16,128]{2,1,0:T(8,128)}, u32[]{:S(2)}) copy-start(f32[16,16,128]{2,1,0:T(8,128)} %slice_multiply_fusion.2) | copy-start | bytes 393220
where the time goes:
time: 252 us; the launch traced here: 248 us
  other arithmetic  74.9 us (30%)
  waiting for transfers between devices  59 us (23%)
  blocking collectives  44.7 us (18%)
  starting transfers between devices  35.7 us (14%)
  local copies, waits for them, and re-layouts  32.2 us (13%)
    psum x5, blocking collectives, over_axes(): shard = lax.psum(shard, axis)  44.7 us
    ppermute x6, waiting for transfers between devices, with_halo(): before = lax.ppermute(last, axis, up)  31.5 us
    mul x3, other arithmetic, shards(): flux = trim_to(conduct_wide, outer - margin) * adjoint  29 us
    ppermute x6, waiting for transfers between devices, with_halo(): after = lax.ppermute(leading, axis, down)  27.5 us
    ppermute x6, starting transfers between devices, with_halo(): after = lax.ppermute(leading, axis, down)  21.1 us
    add x2, other arithmetic, shards(): inner + cheb_w[step] * (trim_to(source_wide, cut) - applied) / diag_here  14.8 us
    ppermute x6, starting transfers between devices, with_halo(): before = lax.ppermute(last, axis, up)  14.6 us
    concatenate x3, other arithmetic, with_halo(): shard = jnp.concatenate([before, shard, after], axis=dim)  9.32 us
  transfers between devices with their start and end apart: 12, of which 8 were waited for; matrix products, arithmetic and copies ran while one was open for 3% of the time, Pallas kernels for 0%

commit v1 on v0

--- a/solution.py
+++ b/solution.py
@@ -29,7 +29,7 @@
 
 def over_axes(shard, axes):
     for axis in axes:
-        shard = lax.psum(shard, axis)
+        shard = jnp.sum(lax.all_gather(shard, axis), axis=0)
     return shard
 
 

time: 252 us -> 254 us (level)
  waiting for transfers between devices: 59 us -> 52.7 us
  local copies, waits for them, and re-layouts: 32.2 us -> 36.8 us
  between operations: 1.51 us -> 4.82 us
    psum x5 -> x0, blocking collectives: 44.7 us -> none  [over_axes(): shard = lax.psum(shard, axis)]
    unnamed x0 -> x5, blocking collectives: none -> 44.6 us
    unnamed x68 -> x93, local copies, waits for them, and re-layouts: 1.66 us -> 5.78 us
    ppermute x6, waiting for transfers between devices: 31.5 us -> 27.8 us  [with_halo(): before = lax.ppermute(last, axis, up)]
    ppermute x6, waiting for transfers between devices: 27.5 us -> 24.9 us  [with_halo(): after = lax.ppermute(leading, axis, down)]
  transfers between devices with their start and end apart: 12 -> 12, of which waited for: 8 -> 7; matrix products, arithmetic and copies ran while one was open for 3% -> 5% of each run, Pallas kernels for 0% -> 0%
where the time goes in v1:
time: 254 us; the launch traced here: 250 us
  other arithmetic  75 us (30%)
  waiting for transfers between devices  52.7 us (21%)
  blocking collectives  44.6 us (18%)
  local copies, waits for them, and re-layouts  36.8 us (14%)
  starting transfers between devices  35.7 us (14%)
  between operations  4.82 us (2%)
    unnamed x5, blocking collectives  44.6 us
    mul x3, other arithmetic, shards(): flux = trim_to(conduct_wide, outer - margin) * adjoint  28.9 us
    ppermute x6, waiting for transfers between devices, with_halo(): before = lax.ppermute(last, axis, up)  27.8 us
    ppermute x6, waiting for transfers between devices, with_halo(): after = lax.ppermute(leading, axis, down)  24.9 us
    ppermute x6, starting transfers between devices, with_halo(): after = lax.ppermute(leading, axis, down)  21.1 us
    add x2, other arithmetic, shards(): inner + cheb_w[step] * (trim_to(source_wide, cut) - applied) / diag_here  14.8 us
    ppermute x6, starting transfers between devices, with_halo(): before = lax.ppermute(last, axis, up)  14.6 us
    concatenate x3, other arithmetic, with_halo(): shard = jnp.concatenate([before, shard, after], axis=dim)  9.32 us
  transfers between devices with their start and end apart: 12, of which 7 were waited for; matrix products, arithmetic and copies ran while one was open for 5% of the time, Pallas kernels for 0%

profile of v1, /device:TPU:6, one launch (start us, length us, event | category | flops | bytes accessed | tf_op | source)
XLA Modules:
  0.0 249.7 jit_solution(10377951148598307721)
XLA Ops:
  2.7 1.9 collective-permute-start
  4.6 1.3 collective-permute-start.1
  6.0 3.5 %collective-permute-done.1 = f32[10,4,16,128]{3,2,1,0:T(8,128)S(1)} collective-permute-done((f32[10,4,16,128]{3,2,1,0:T(8,128)S(1)}, f32[10,4,16,128]{3,2,1,0:T(8,128)S(1)}, u32[]{:S(2)}, u32[]{:S(2)}) %collective-permute-start.1) | collective-permute-done | bytes 327712 | tf_op jit(solution)/shard_map/ppermute | solution.py:25
  9.5 1.5 pad_maximum_fusion.24
  11.1 2.7 %collective-permute-start.3 = (f32[10,24,4,128]{3,1,2,0:T(8,128)S(1)}, f32[10,24,4,128]{3,1,2,0:T(8,128)S(1)}, u32[]{:S(2)}, u32[]{:S(2)}) collective-permute-start(f32[10,24,4,128]{3,1,2,0:T(8,128)S(1)} %copy.40), channel_id=1, source_target_pairs={{2,0},{4,2},{6,4},{8,6},{10,8},{12,10},{14,12},{16,14},{18,16},{20... | collective-permute-start | bytes 1474568 | tf_op jit(solution)/shard_map/ppermute | solution.py:25
  13.9 4.0 %collective-permute-start.2 = (f32[10,24,4,128]{3,1,2,0:T(8,128)S(1)}, f32[10,24,4,128]{3,1,2,0:T(8,128)S(1)}, u32[]{:S(2)}, u32[]{:S(2)}) collective-permute-start(f32[10,24,4,128]{3,1,2,0:T(8,128)S(1)} %copy.39), channel_id=1, source_target_pairs={{0,2},{2,4},{4,6},{6,8},{8,10},{10,12},{12,14},{14,16},{16,18},{18... | collective-permute-start | bytes 1474568 | tf_op jit(solution)/shard_map/ppermute | solution.py:24
  17.9 5.8 %collective-permute-done.3 = f32[10,24,4,128]{3,1,2,0:T(8,128)S(1)} collective-permute-done((f32[10,24,4,128]{3,1,2,0:T(8,128)S(1)}, f32[10,24,4,128]{3,1,2,0:T(8,128)S(1)}, u32[]{:S(2)}, u32[]{:S(2)}) %collective-permute-start.3) | collective-permute-done | bytes 491552 | tf_op jit(solution)/shard_map/ppermute | solution.py:25
  23.9 14.6 %collective-permute-done.2 = f32[10,24,4,128]{3,1,2,0:T(8,128)S(1)} collective-permute-done((f32[10,24,4,128]{3,1,2,0:T(8,128)S(1)}, f32[10,24,4,128]{3,1,2,0:T(8,128)S(1)}, u32[]{:S(2)}, u32[]{:S(2)}) %collective-permute-start.2) | collective-permute-done | bytes 491552 | tf_op jit(solution)/shard_map/ppermute | solution.py:24
  39.9 2.6 %fusion.63 = (f32[10,24,24,4]{3,2,1,0:T(8,128)}, f32[10,24,24,4]{3,2,1,0:T(8,128)S(1)}) fusion(f32[10,24,24,128]{3,2,1,0:T(8,128)S(1)} %pad_maximum_fusion.2), kind=kLoop, calls=%fused_computation.145 | loop fusion | bytes 368640 | tf_op jit(solution)/shard_map/slice | solution.py:23
  42.5 3.7 %copy.44 = f32[10,24,24,4]{2,1,3,0:T(8,128)} copy(f32[10,24,24,4]{3,2,1,0:T(8,128)} %get-tuple-element.17) | data formatting | bytes 184320 | tf_op jit(solution)/shard_map/slice | solution.py:23
  46.2 2.5 copy.43
  48.7 1.3 collective-permute-start.4
  49.9 8.0 %collective-permute-start.5 = (f32[10,24,24,4]{2,1,3,0:T(8,128)}, f32[10,24,24,4]{2,1,3,0:T(8,128)}, u32[]{:S(2)}, u32[]{:S(2)}) collective-permute-start(f32[10,24,24,4]{2,1,3,0:T(8,128)} %copy.44), channel_id=1, source_target_pairs={{1,0},{3,2},{5,4},{7,6},{9,8},{11,10},{13,12},{15,14},{17,16},{19,... | collective-permute-start | bytes 276488 | tf_op jit(solution)/shard_map/ppermute | solution.py:25
  57.9 1.6 convert_multiply_fusion
  59.5 8.1 %collective-permute-done.5 = f32[10,24,24,4]{2,1,3,0:T(8,128)} collective-permute-done((f32[10,24,24,4]{2,1,3,0:T(8,128)}, f32[10,24,24,4]{2,1,3,0:T(8,128)}, u32[]{:S(2)}, u32[]{:S(2)}) %collective-permute-start.5) | collective-permute-done | bytes 92192 | tf_op jit(solution)/shard_map/ppermute | solution.py:25
  67.6 2.5 copy.46
  70.1 3.9 %copy.45 = f32[10,24,24,4]{3,2,1,0:T(8,128)} copy(f32[10,24,24,4]{2,1,3,0:T(8,128)} %collective-permute-done.4) | data formatting | bytes 184320 | tf_op jit(solution)/shard_map/ppermute | solution.py:24
  74.1 8.5 %pad_maximum_fusion = f32[10,24,24,136]{3,2,1,0:T(8,128)S(1)} fusion(f32[10,24,24,4]{3,2,1,0:T(8,128)S(1)} %copy.46, f32[10,24,4,128]{3,2,1,0:T(4,128)S(1)} %copy.42, f32[10,4,16,128]{3,2,1,0:T(8,128)} %copy-done.12, f32[8,16,16,128]{3,2,1,0:T(8,128)} %param.4, f32[1,16,16,128]{3,2,1,0:T(8,128)} %copy-done.14, f32[1,16,16,128]{3,2,1,0:T(8,128)} %bitcast.14, ...), kind=kLoop, calls=%fused_computation | loop fusion | flops 6266880 | bytes 6266880 | tf_op jit(solution)/shard_map/concatenate | solution.py:26
  83.2 1.9 fusion.66
  85.6 1.4 multiply_divide_fusion.1
  87.1 7.5 %fusion.11 = f32[8,20,20,132]{3,2,1,0:T(8,128)S(1)} fusion(f32[8,22,22,134]{3,2,1,0:T(8,128)S(1)} %get-tuple-element.13, f32[8,22,22,134]{3,2,1,0:T(8,128)S(1)} %get-tuple-element.14, f32[20,20,132]{2,1,0:T(8,128)S(1)} %slice.379, f32[20,20,132]{2,1,0:T(8,128)S(1)} %slice.378), kind=kLoop, calls=%fused_computation.26 | loop fusion | flops 5068800 | bytes 15628800 | tf_op jit(solution)/shard_map/add | solution.py:80
  94.6 7.3 %fusion.22 = f32[8,18,18,130]{3,2,1,0:T(8,128)S(1)} fusion(f32[8,20,20,132]{3,2,1,0:T(8,128)S(1)} %fusion.11, f32[8,22,22,134]{3,2,1,0:T(8,128)S(1)} %get-tuple-element.14, f32[18,18,130]{2,1,0:T(8,128)S(1)} %slice.389, f32[18,18,130]{2,1,0:T(8,128)S(1)} %slice.388), kind=kLoop, calls=%fused_computation.47 | loop fusion | flops 4043520 | bytes 12467520 | tf_op jit(solution)/shard_map/add | solution.py:80
  101.9 2.9 %fusion.57 = f32[8,16,16,128]{3,2,1,0:T(8,128)} fusion(f32[8,18,18,130]{3,2,1,0:T(8,128)S(1)} %fusion.22, f32[8,22,22,134]{3,2,1,0:T(8,128)S(1)} %get-tuple-element.14, f32[16,16,128]{2,1,0:T(8,128)S(1)} %slice.399, f32[16,16,128]{2,1,0:T(8,128)S(1)} %slice.398, f32[16,16,128]{2,1,0:T(8,128)S(1)} %copy-done.33), kind=kLoop, calls=%fused_computation.118 | loop fusion | flops 3407872 | bytes 9830400 | tf_op jit(solution)/shard_map/mul | solution.py:81
  106.0 1.3 collective-permute-start.6
  107.3 1.3 collective-permute-start.7
  108.7 7.4 %collective-permute-done.7 = f32[8,3,16,128]{3,2,1,0:T(8,128)S(1)} collective-permute-done((f32[8,3,16,128]{3,2,1,0:T(8,128)S(1)}, f32[8,3,16,128]{3,2,1,0:T(8,128)S(1)}, u32[]{:S(2)}, u32[]{:S(2)}) %collective-permute-start.7) | collective-permute-done | bytes 196640 | tf_op jit(solution)/shard_map/ppermute | solution.py:25
  116.0 1.4 pad_maximum_fusion.27
  117.5 1.9 collective-permute-start.9
  119.5 4.8 %collective-permute-start.8 = (f32[8,22,3,128]{3,0,2,1:T(8,128)S(1)}, f32[8,22,3,128]{3,0,2,1:T(8,128)S(1)}, u32[]{:S(2)}, u32[]{:S(2)}) collective-permute-start(f32[8,22,3,128]{3,0,2,1:T(8,128)S(1)} %copy.47), channel_id=1, source_target_pairs={{0,2},{2,4},{4,6},{6,8},{8,10},{10,12},{12,14},{14,16},{16,18},{18... | collective-permute-start | bytes 811016 | tf_op jit(solution)/shard_map/ppermute | solution.py:24
  130.7 4.5 %collective-permute-done.8 = f32[8,22,3,128]{3,0,2,1:T(8,128)S(1)} collective-permute-done((f32[8,22,3,128]{3,0,2,1:T(8,128)S(1)}, f32[8,22,3,128]{3,0,2,1:T(8,128)S(1)}, u32[]{:S(2)}, u32[]{:S(2)}) %collective-permute-start.8) | collective-permute-done | bytes 270368 | tf_op jit(solution)/shard_map/ppermute | solution.py:24
  136.4 2.0 fusion.64
  138.5 1.8 copy.51
  140.3 2.8 %copy.52 = f32[8,22,22,3]{2,0,3,1:T(8,128)S(1)} copy(f32[8,22,22,3]{3,2,1,0:T(8,128)} %get-tuple-element.20) | data formatting | bytes 92928 | tf_op jit(solution)/shard_map/slice | solution.py:23
  143.2 5.9 %collective-permute-start.11 = (f32[8,22,22,3]{2,0,3,1:T(8,128)S(1)}, f32[8,22,22,3]{2,0,3,1:T(8,128)S(1)}, u32[]{:S(2)}, u32[]{:S(2)}) collective-permute-start(f32[8,22,22,3]{2,0,3,1:T(8,128)S(1)} %copy.52), channel_id=1, source_target_pairs={{1,0},{3,2},{5,4},{7,6},{9,8},{11,10},{13,12},{15,14},{17,16},{19,... | collective-permute-start | bytes 139400 | tf_op jit(solution)/shard_map/ppermute | solution.py:25
  149.1 1.3 collective-permute-start.10
  150.4 1.8 slice_multiply_fusion.2
  152.2 8.7 %collective-permute-done.10 = f32[8,22,22,3]{2,0,3,1:T(8,128)S(1)} collective-permute-done((f32[8,22,22,3]{2,0,3,1:T(8,128)}, f32[8,22,22,3]{2,0,3,1:T(8,128)S(1)}, u32[]{:S(2)}, u32[]{:S(2)}) %collective-permute-start.10) | collective-permute-done | bytes 46496 | tf_op jit(solution)/shard_map/ppermute | solution.py:24
  160.9 2.5 copy.53
  163.4 2.5 copy.54
  165.9 8.0 %broadcast_multiply_fusion = (f32[8,22,22,134]{3,2,1,0:T(8,128)S(1)}, f32[8,22,22,134]{3,2,1,0:T(8,128)}, f32[8,22,22,134]{3,2,1,0:T(8,128)S(1)}) fusion(f32[22,22,134]{2,1,0:T(8,128)} %get-tuple-element.29, f32[22,22,134]{2,1,0:T(8,128)S(1)} %copy-done.5, f32[8,22,22,3]{3,2,1,0:T(8,128)} %copy.54, f32[8,22,3,128]{3,2,1,0:T(4,128)S(1)} %copy-done.25, ...), kind=kLoop, calls=%fused_computation.54 | loop fusion | flops 4669632 | bytes 8820416 | tf_op jit(solution)/shard_map/mul | solution.py:86
  173.9 10.7 %broadcast_multiply_fusion.1 = (f32[8,20,20,132]{3,2,1,0:T(8,128)S(1)}, f32[8,20,20,132]{3,2,1,0:T(8,128)}) fusion(f32[20,20,132]{2,1,0:T(8,128)S(1)} %copy-done.17, f32[8,22,22,134]{3,2,1,0:T(8,128)S(1)} %get-tuple-element.10, f32[20,20,132]{2,1,0:T(8,128)S(1)} %copy-done.19, f32[8,22,22,134]{3,2,1,0:T(8,128)S(1)} %get-tuple-element.12, ...), kind=kLoop, calls=%fused_computation.55 | loop fusion | flops 5068800 | bytes 17318400 | tf_op jit(solution)/shard_map/mul | solution.py:86
  184.6 10.3 %broadcast_multiply_fusion.2 = (f32[8,18,18,130]{3,2,1,0:T(8,128)S(1)}, f32[8,18,18,130]{3,2,1,0:T(8,128)}) fusion(f32[18,18,130]{2,1,0:T(8,128)} %copy-done.20, f32[8,20,20,132]{3,2,1,0:T(8,128)S(1)} %get-tuple-element.8, f32[18,18,130]{2,1,0:T(8,128)} %copy-done.21, f32[8,22,22,134]{3,2,1,0:T(8,128)S(1)} %get-tuple-element.12, ...), kind=kLoop, calls=%fused_computation.56 | loop fusion | flops 4043520 | bytes 13815360 | tf_op jit(solution)/shard_map/mul | solution.py:86
  195.0 7.7 %multiply_reduce_fusion = (f32[8]{0:T(128)S(1)}, f32[8,16,16,128]{3,2,1,0:T(8,128)}) fusion(f32[8,16,16,128]{3,2,1,0:T(8,128)S(1)} %copy-done.3, f32[10,24,4,128]{3,2,1,0:T(4,128)S(1)} %copy-done.7, f32[10,4,16,128]{3,2,1,0:T(8,128)S(1)} %copy-done.13, f32[1,16,16,128]{3,2,1,0:T(8,128)S(1)} %copy-done.15, f32[1,16,16,128]{3,2,1,0:T(8,128)S(1)} %bitcast.16, ...), kind=kLoop, calls=%fused_computation.117 | loop fusion | flops 13893624 | bytes 12832800 | tf_op jit(solution)/shard_map/reduce_sum | solution.py:106
  202.8 11.8 %all-reduce = f32[32]{0:T(128)S(1)} all-reduce(f32[32]{0:T(128)S(1)} %dynamic-update-slice), channel_id=2, replica_groups=mesh['gx_0'=4,'gx_1'=2,'gy_0'=8,'gy_1'=2,'gz'=2] {'gx_0'}, use_global_device_ids=true, to_apply=%add | all-reduce | flops 32 | bytes 256
  215.0 2.4 all-reduce.1
  217.8 19.1 %all-reduce.2 = f32[64]{0:T(128)S(1)} all-reduce(f32[64]{0:T(128)S(1)} %dynamic-update-slice.2), channel_id=4, replica_groups=mesh['gx_0'=4,'gx_1'=2,'gy_0'=8,'gy_1'=2,'gz'=2] {'gy_0'}, use_global_device_ids=true, to_apply=%add.2 | all-reduce | flops 64 | bytes 512
  237.2 4.9 %all-reduce.3 = f32[16]{0:T(128)S(1)} all-reduce(f32[16]{0:T(128)S(1)} %dynamic-update-slice.3), channel_id=5, replica_groups=mesh['gx_0'=4,'gx_1'=2,'gy_0'=8,'gy_1'=2,'gz'=2] {'gy_1'}, use_global_device_ids=true, to_apply=%add.3 | all-reduce | flops 16 | bytes 128
  242.5 6.4 %all-reduce.4 = f32[16]{0:T(128)S(1)} all-reduce(f32[16]{0:T(128)S(1)} %dynamic-update-slice.4), channel_id=6, replica_groups=mesh['gx_0'=4,'gx_1'=2,'gy_0'=8,'gy_1'=2,'gz'=2] {'gz'}, use_global_device_ids=true, to_apply=%add.4 | all-reduce | flops 16 | bytes 128
  (129 shorter events, 12.5 us)
Async XLA Ops:
  1.6 37.0 %copy-start.14 = (f32[1,16,16,128]{3,2,1,0:T(8,128)}, f32[1,16,16,128]{3,2,1,0:T(8,128)S(1)}, u32[]{:S(2)}) copy-start(f32[1,16,16,128]{3,2,1,0:T(8,128)S(1)} %exponential_bitcast_fusion) | copy-start | bytes 393220
  2.7 36.6 %copy-start.2 = (f32[8,16,16,128]{3,2,1,0:T(8,128)S(1)}, f32[8,16,16,128]{3,2,1,0:T(8,128)}, u32[]{:S(2)}) copy-start(f32[8,16,16,128]{3,2,1,0:T(8,128)} %param.4) | copy-start | bytes 3145732
  2.7 36.6 %copy-start.22 = (f32[16,16,128]{2,1,0:T(8,128)S(1)}, f32[16,16,128]{2,1,0:T(8,128)}, u32[]{:S(2)}) copy-start(f32[16,16,128]{2,1,0:T(8,128)} %param.5) | copy-start | bytes 393220
  2.7 3.2 %collective-permute-start = (f32[10,4,16,128]{3,2,1,0:T(8,128)S(1)}, f32[10,4,16,128]{3,2,1,0:T(8,128)S(1)}, u32[]{:S(2)}, u32[]{:S(2)}) collective-permute-start(f32[10,4,16,128]{3,2,1,0:T(8,128)S(1)} %get-tuple-element.25), channel_id=1, source_target_pairs={{0,32},{32,64},{64,96},{96,128},{128,160},{160,192},{192,224},{1,3... | collective-permute-start | bytes 983048 | tf_op jit(solution)/shard_map/ppermute | solution.py:24
  4.6 4.9 %collective-permute-start.1 = (f32[10,4,16,128]{3,2,1,0:T(8,128)S(1)}, f32[10,4,16,128]{3,2,1,0:T(8,128)S(1)}, u32[]{:S(2)}, u32[]{:S(2)}) collective-permute-start(f32[10,4,16,128]{3,2,1,0:T(8,128)S(1)} %get-tuple-element.26), channel_id=1, source_target_pairs={{32,0},{64,32},{96,64},{128,96},{160,128},{192,160},{224,192},{33,... | collective-permute-start | bytes 983048 | tf_op jit(solution)/shard_map/ppermute | solution.py:25
  5.9 33.9 %copy-start.10 = (f32[10,4,16,128]{3,2,1,0:T(8,128)}, f32[10,4,16,128]{3,2,1,0:T(8,128)S(1)}, u32[]{:S(2)}) copy-start(f32[10,4,16,128]{3,2,1,0:T(8,128)S(1)} %collective-permute-done) | copy-start | bytes 983044
  9.5 30.3 %copy-start.12 = (f32[10,4,16,128]{3,2,1,0:T(8,128)}, f32[10,4,16,128]{3,2,1,0:T(8,128)S(1)}, u32[]{:S(2)}) copy-start(f32[10,4,16,128]{3,2,1,0:T(8,128)S(1)} %collective-permute-done.1) | copy-start | bytes 983044
  11.1 12.6 %collective-permute-start.3 = (f32[10,24,4,128]{3,1,2,0:T(8,128)S(1)}, f32[10,24,4,128]{3,1,2,0:T(8,128)S(1)}, u32[]{:S(2)}, u32[]{:S(2)}) collective-permute-start(f32[10,24,4,128]{3,1,2,0:T(8,128)S(1)} %copy.40), channel_id=1, source_target_pairs={{2,0},{4,2},{6,4},{8,6},{10,8},{12,10},{14,12},{16,14},{18,16},{20... | collective-permute-start | bytes 1474568 | tf_op jit(solution)/shard_map/ppermute | solution.py:25
  13.9 24.5 %collective-permute-start.2 = (f32[10,24,4,128]{3,1,2,0:T(8,128)S(1)}, f32[10,24,4,128]{3,1,2,0:T(8,128)S(1)}, u32[]{:S(2)}, u32[]{:S(2)}) collective-permute-start(f32[10,24,4,128]{3,1,2,0:T(8,128)S(1)} %copy.39), channel_id=1, source_target_pairs={{0,2},{2,4},{4,6},{6,8},{8,10},{10,12},{12,14},{14,16},{16,18},{18... | collective-permute-start | bytes 1474568 | tf_op jit(solution)/shard_map/ppermute | solution.py:24
  23.9 50.2 %copy-start.6 = (f32[10,24,4,128]{3,2,1,0:T(4,128)}, f32[10,24,4,128]{3,2,1,0:T(4,128)S(1)}, u32[]{:S(2)}) copy-start(f32[10,24,4,128]{3,2,1,0:T(4,128)S(1)} %copy.42) | copy-start | bytes 1474564
  48.7 21.5 %collective-permute-start.4 = (f32[10,24,24,4]{2,1,3,0:T(8,128)}, f32[10,24,24,4]{2,1,3,0:T(8,128)}, u32[]{:S(2)}, u32[]{:S(2)}) collective-permute-start(f32[10,24,24,4]{2,1,3,0:T(8,128)} %copy.43), channel_id=1, source_target_pairs={{0,1},{2,3},{4,5},{6,7},{8,9},{10,11},{12,13},{14,15},{16,17},{18,... | collective-permute-start | bytes 276488 | tf_op jit(solution)/shard_map/ppermute | solution.py:24
  49.9 17.7 %collective-permute-start.5 = (f32[10,24,24,4]{2,1,3,0:T(8,128)}, f32[10,24,24,4]{2,1,3,0:T(8,128)}, u32[]{:S(2)}, u32[]{:S(2)}) collective-permute-start(f32[10,24,24,4]{2,1,3,0:T(8,128)} %copy.44), channel_id=1, source_target_pairs={{1,0},{3,2},{5,4},{7,6},{9,8},{11,10},{13,12},{15,14},{17,16},{19,... | collective-permute-start | bytes 276488 | tf_op jit(solution)/shard_map/ppermute | solution.py:25
  70.1 12.5 %copy-start.1 = (f32[10,24,24,4]{3,2,1,0:T(8,128)}, f32[10,24,24,4]{3,2,1,0:T(8,128)S(1)}, u32[]{:S(2)}) copy-start(f32[10,24,24,4]{3,2,1,0:T(8,128)S(1)} %copy.46) | copy-start | bytes 276484
  83.0 11.6 %copy-start.20 = (f32[18,18,130]{2,1,0:T(8,128)}, f32[18,18,130]{2,1,0:T(8,128)S(1)}, u32[]{:S(2)}) copy-start(f32[18,18,130]{2,1,0:T(8,128)S(1)} %slice.389) | copy-start | bytes 505444
  83.2 3.9 %copy-start.16 = (f32[20,20,132]{2,1,0:T(8,128)}, f32[20,20,132]{2,1,0:T(8,128)S(1)}, u32[]{:S(2)}) copy-start(f32[20,20,132]{2,1,0:T(8,128)S(1)} %slice.379) | copy-start | bytes 633604
  85.0 2.0 copy-start.4
  85.0 2.0 copy-start.28
  85.2 16.8 %copy-start.30 = (f32[16,16,128]{2,1,0:T(8,128)}, f32[16,16,128]{2,1,0:T(8,128)S(1)}, u32[]{:S(2)}) copy-start(f32[16,16,128]{2,1,0:T(8,128)S(1)} %slice.398) | copy-start | bytes 393220
  85.4 9.2 %copy-start.21 = (f32[18,18,130]{2,1,0:T(8,128)}, f32[18,18,130]{2,1,0:T(8,128)S(1)}, u32[]{:S(2)}) copy-start(f32[18,18,130]{2,1,0:T(8,128)S(1)} %slice.388) | copy-start | bytes 505444
  94.6 7.3 %copy-start.33 = (f32[16,16,128]{2,1,0:T(8,128)S(1)}, f32[16,16,128]{2,1,0:T(8,128)}, u32[]{:S(2)}) copy-start(f32[16,16,128]{2,1,0:T(8,128)} %convert_multiply_fusion) | copy-start | bytes 393220
  104.9 19.5 %copy-start.38 = (u32[256]{0:T(256)S(1)}, u32[256]{0:T(256)}, u32[]{:S(2)}) copy-start(u32[256]{0:T(256)} %constant.44) | copy-start | bytes 3076
  104.9 20.1 %copy-start.37 = (u32[256]{0:T(256)S(1)}, u32[256]{0:T(256)}, u32[]{:S(2)}) copy-start(u32[256]{0:T(256)} %constant.39) | copy-start | bytes 3076
  104.9 22.0 %copy-start.36 = (u32[256]{0:T(256)S(1)}, u32[256]{0:T(256)}, u32[]{:S(2)}) copy-start(u32[256]{0:T(256)} %constant.34) | copy-start | bytes 3076
  104.9 23.2 %copy-start.35 = (u32[256]{0:T(256)S(1)}, u32[256]{0:T(256)}, u32[]{:S(2)}) copy-start(u32[256]{0:T(256)} %constant.29) | copy-start | bytes 3076
  104.9 24.5 %copy-start.34 = (u32[256]{0:T(256)S(1)}, u32[256]{0:T(256)}, u32[]{:S(2)}) copy-start(u32[256]{0:T(256)} %constant.24) | copy-start | bytes 3076
  104.9 31.2 %copy-start = (f32[8,16,16,128]{3,2,1,0:T(8,128)S(1)}, f32[8,16,16,128]{3,2,1,0:T(8,128)}, u32[]{:S(2)}) copy-start(f32[8,16,16,128]{3,2,1,0:T(8,128)} %fusion.57) | copy-start | bytes 3145732
  106.0 2.6 %collective-permute-start.6 = (f32[8,3,16,128]{3,2,1,0:T(8,128)S(1)}, f32[8,3,16,128]{3,2,1,0:T(8,128)S(1)}, u32[]{:S(2)}, u32[]{:S(2)}) collective-permute-start(f32[8,3,16,128]{3,2,1,0:T(8,128)S(1)} %get-tuple-element.27), channel_id=1, source_target_pairs={{0,32},{32,64},{64,96},{96,128},{128,160},{160,192},{192,224},{1,3... | collective-permute-start | bytes 589832 | tf_op jit(solution)/shard_map/ppermute | solution.py:24
  107.3 8.7 %collective-permute-start.7 = (f32[8,3,16,128]{3,2,1,0:T(8,128)S(1)}, f32[8,3,16,128]{3,2,1,0:T(8,128)S(1)}, u32[]{:S(2)}, u32[]{:S(2)}) collective-permute-start(f32[8,3,16,128]{3,2,1,0:T(8,128)S(1)} %get-tuple-element.28), channel_id=1, source_target_pairs={{32,0},{64,32},{96,64},{128,96},{160,128},{192,160},{224,192},{33,... | collective-permute-start | bytes 589832 | tf_op jit(solution)/shard_map/ppermute | solution.py:25
  116.0 19.2 %copy-start.29 = (f32[8,3,16,128]{3,2,1,0:T(8,128)}, f32[8,3,16,128]{3,2,1,0:T(8,128)S(1)}, u32[]{:S(2)}) copy-start(f32[8,3,16,128]{3,2,1,0:T(8,128)S(1)} %collective-permute-done.7) | copy-start | bytes 589828
  117.5 13.0 %collective-permute-start.9 = (f32[8,22,3,128]{3,0,2,1:T(8,128)S(1)}, f32[8,22,3,128]{3,0,2,1:T(8,128)S(1)}, u32[]{:S(2)}, u32[]{:S(2)}) collective-permute-start(f32[8,22,3,128]{3,0,2,1:T(8,128)S(1)} %copy.48), channel_id=1, source_target_pairs={{2,0},{4,2},{6,4},{8,6},{10,8},{12,10},{14,12},{16,14},{18,16},{20... | collective-permute-start | bytes 811016 | tf_op jit(solution)/shard_map/ppermute | solution.py:25
  119.5 15.7 %collective-permute-start.8 = (f32[8,22,3,128]{3,0,2,1:T(8,128)S(1)}, f32[8,22,3,128]{3,0,2,1:T(8,128)S(1)}, u32[]{:S(2)}, u32[]{:S(2)}) collective-permute-start(f32[8,22,3,128]{3,0,2,1:T(8,128)S(1)} %copy.47), channel_id=1, source_target_pairs={{0,2},{2,4},{4,6},{6,8},{8,10},{10,12},{12,14},{14,16},{16,18},{18... | collective-permute-start | bytes 811016 | tf_op jit(solution)/shard_map/ppermute | solution.py:24
  130.7 4.6 %copy-start.24 = (f32[8,22,3,128]{3,2,1,0:T(4,128)}, f32[8,22,3,128]{3,2,1,0:T(4,128)S(1)}, u32[]{:S(2)}) copy-start(f32[8,22,3,128]{3,2,1,0:T(4,128)S(1)} %copy.50) | copy-start | bytes 811012
  140.3 25.6 %copy-start.5 = (f32[22,22,134]{2,1,0:T(8,128)S(1)}, f32[22,22,134]{2,1,0:T(8,128)}, u32[]{:S(2)}) copy-start(f32[22,22,134]{2,1,0:T(8,128)} %copy-done.4) | copy-start | bytes 778276
  140.3 25.6 %copy-start.25 = (f32[8,22,3,128]{3,2,1,0:T(4,128)S(1)}, f32[8,22,3,128]{3,2,1,0:T(4,128)}, u32[]{:S(2)}) copy-start(f32[8,22,3,128]{3,2,1,0:T(4,128)} %copy-done.24) | copy-start | bytes 811012
  140.3 25.6 %copy-start.27 = (f32[8,22,3,128]{3,2,1,0:T(4,128)S(1)}, f32[8,22,3,128]{3,2,1,0:T(4,128)}, u32[]{:S(2)}) copy-start(f32[8,22,3,128]{3,2,1,0:T(4,128)} %copy-done.26) | copy-start | bytes 811012
  143.2 20.2 %collective-permute-start.11 = (f32[8,22,22,3]{2,0,3,1:T(8,128)S(1)}, f32[8,22,22,3]{2,0,3,1:T(8,128)S(1)}, u32[]{:S(2)}, u32[]{:S(2)}) collective-permute-start(f32[8,22,22,3]{2,0,3,1:T(8,128)S(1)} %copy.52), channel_id=1, source_target_pairs={{1,0},{3,2},{5,4},{7,6},{9,8},{11,10},{13,12},{15,14},{17,16},{19,... | collective-permute-start | bytes 139400 | tf_op jit(solution)/shard_map/ppermute | solution.py:25
  149.1 11.8 %collective-permute-start.10 = (f32[8,22,22,3]{2,0,3,1:T(8,128)}, f32[8,22,22,3]{2,0,3,1:T(8,128)S(1)}, u32[]{:S(2)}, u32[]{:S(2)}) collective-permute-start(f32[8,22,22,3]{2,0,3,1:T(8,128)} %copy.51), channel_id=1, source_target_pairs={{0,1},{2,3},{4,5},{6,7},{8,9},{10,11},{12,13},{14,15},{16,17},{18,... | collective-permute-start | bytes 139400 | tf_op jit(solution)/shard_map/ppermute | solution.py:24
  165.9 8.0 %copy-start.17 = (f32[20,20,132]{2,1,0:T(8,128)S(1)}, f32[20,20,132]{2,1,0:T(8,128)}, u32[]{:S(2)}) copy-start(f32[20,20,132]{2,1,0:T(8,128)} %copy-done.16) | copy-start | bytes 633604
  165.9 8.0 %copy-start.19 = (f32[20,20,132]{2,1,0:T(8,128)S(1)}, f32[20,20,132]{2,1,0:T(8,128)}, u32[]{:S(2)}) copy-start(f32[20,20,132]{2,1,0:T(8,128)} %copy-done.18) | copy-start | bytes 633604
  184.5 10.3 %copy-start.3 = (f32[8,16,16,128]{3,2,1,0:T(8,128)S(1)}, f32[8,16,16,128]{3,2,1,0:T(8,128)}, u32[]{:S(2)}) copy-start(f32[8,16,16,128]{3,2,1,0:T(8,128)} %param.4) | copy-start | bytes 3145732
  184.6 10.3 %copy-start.7 = (f32[10,24,4,128]{3,2,1,0:T(4,128)S(1)}, f32[10,24,4,128]{3,2,1,0:T(4,128)}, u32[]{:S(2)}) copy-start(f32[10,24,4,128]{3,2,1,0:T(4,128)} %copy-done.6) | copy-start | bytes 1474564
  184.6 10.3 %copy-start.9 = (f32[10,24,4,128]{3,2,1,0:T(4,128)S(1)}, f32[10,24,4,128]{3,2,1,0:T(4,128)}, u32[]{:S(2)}) copy-start(f32[10,24,4,128]{3,2,1,0:T(4,128)} %copy-done.8) | copy-start | bytes 1474564
  184.6 10.3 %copy-start.11 = (f32[10,4,16,128]{3,2,1,0:T(8,128)S(1)}, f32[10,4,16,128]{3,2,1,0:T(8,128)}, u32[]{:S(2)}) copy-start(f32[10,4,16,128]{3,2,1,0:T(8,128)} %copy-done.10) | copy-start | bytes 983044
  184.6 10.3 %copy-start.13 = (f32[10,4,16,128]{3,2,1,0:T(8,128)S(1)}, f32[10,4,16,128]{3,2,1,0:T(8,128)}, u32[]{:S(2)}) copy-start(f32[10,4,16,128]{3,2,1,0:T(8,128)} %copy-done.12) | copy-start | bytes 983044
  184.6 10.3 %copy-start.15 = (f32[1,16,16,128]{3,2,1,0:T(8,128)S(1)}, f32[1,16,16,128]{3,2,1,0:T(8,128)}, u32[]{:S(2)}) copy-start(f32[1,16,16,128]{3,2,1,0:T(8,128)} %copy-done.14) | copy-start | bytes 393220
  184.6 10.3 %copy-start.23 = (f32[16,16,128]{2,1,0:T(8,128)S(1)}, f32[16,16,128]{2,1,0:T(8,128)}, u32[]{:S(2)}) copy-start(f32[16,16,128]{2,1,0:T(8,128)} %param.5) | copy-start | bytes 393220
  184.6 10.3 %copy-start.31 = (f32[16,16,128]{2,1,0:T(8,128)S(1)}, f32[16,16,128]{2,1,0:T(8,128)}, u32[]{:S(2)}) copy-start(f32[16,16,128]{2,1,0:T(8,128)} %copy-done.30) | copy-start | bytes 393220
  184.6 10.3 %copy-start.32 = (f32[16,16,128]{2,1,0:T(8,128)S(1)}, f32[16,16,128]{2,1,0:T(8,128)}, u32[]{:S(2)}) copy-start(f32[16,16,128]{2,1,0:T(8,128)} %slice_multiply_fusion.2) | copy-start | bytes 393220
  (3 other events, 3.0 us)
